TPU v7x, 32 devices: a whole 2x2x4 slice. The times are simulated.
32 devices in a mesh: node: 4 (over y, core), rep: 8 (over z, x).
Axes of the slice: x: 2, y: 2, z: 4, core: 2. Of those that a mesh axis runs over, the one named last changes fastest.
Arguments:
- tokens: bfloat16 [8192, 2048], P(('node', 'rep')), may hold values from -60 to 60
- cotangent: bfloat16 [8192, 512], P(('node', 'rep')), may hold values from -6 to 6
- value_weight: bfloat16 [2048, 512], P('node'), may hold values from -0.25 to 0.25
Outputs:
- input_grad: bfloat16 [8192, 2048], P(('node', 'rep'))
- update: float32 [2048, 512], P('node')
All inputs are finite; a program needn't handle non-finite values.
Results may differ from a plain program's by a relative error of at most 0.025.
Values may be sent and summed in bfloat16 or wider, within the bound.
A program may use at most 64 MiB of HBM per device.

v0:
```python
import math

import jax
import jax.numpy as jnp
from jax import lax
from jax.sharding import PartitionSpec as P

DIN = 2048
HD = 128
NS_ITERS = 5


coef_a = 3.4445
coef_b = -4.775
coef_c = 2.0315
epsilon = 1e-07


def per_device(tokens, cotangent, value_weight):
    width = value_weight.shape[1]
    local_rows = value_weight.shape[0]
    heads = width // HD
    input_grad = lax.dot_general(
        cotangent,
        lax.all_gather(value_weight, "node", axis=0, tiled=True),
        (((1,), (1,)), ((), ())),
        preferred_element_type=jnp.float32,
    ).astype(jnp.bfloat16)
    partial_rows = lax.psum_scatter(
        lax.dot_general(
            tokens, cotangent, (((0,), (0,)), ((), ())), preferred_element_type=jnp.float32
        ).astype(jnp.bfloat16),
        "node",
        scatter_dimension=0,
        tiled=True,
    ).astype(jnp.float32)
    gradient = lax.psum(partial_rows, "rep")
    blocks = gradient.reshape(local_rows, heads, HD)
    local_raw = jnp.einsum("rhi,rhj->hij", blocks, blocks, precision=lax.Precision.HIGHEST)
    gram_raw = lax.psum(local_raw, "node")
    squares = jnp.einsum("hii->h", gram_raw)
    divisor = jnp.sqrt(squares) + epsilon
    start_iterate = blocks / divisor[None, :, None]
    gram = gram_raw / (divisor * divisor)[:, None, None]
    identity = jnp.broadcast_to(jnp.eye(HD, dtype=jnp.float32), (heads, HD, HD))
    total = identity
    for step in range(NS_ITERS):
        factor = (
            coef_a * identity
            + coef_b * gram
            + coef_c * jnp.einsum("hij,hjk->hik", gram, gram, precision=lax.Precision.HIGHEST)
        )
        total = jnp.einsum("hij,hjk->hik", total, factor, precision=lax.Precision.HIGHEST)
        if step + 1 < NS_ITERS:
            halfway = jnp.einsum("hij,hjk->hik", gram, factor, precision=lax.Precision.HIGHEST)
            gram = jnp.einsum("hji,hjk->hik", factor, halfway, precision=lax.Precision.HIGHEST)
    iterate = jnp.einsum("rhi,hij->rhj", start_iterate, total, precision=lax.Precision.HIGHEST)
    update = 0.2 * math.sqrt(DIN) * iterate.reshape(local_rows, width)
    return (input_grad, update)


def solution(mesh):
    in_specs = (P(("node", "rep"), None), P(("node", "rep"), None), P("node", None))
    out_specs = (P(("node", "rep"), None), P("node", None))
    return jax.shard_map(
        per_device, mesh=mesh, in_specs=in_specs, out_specs=out_specs, check_vma=False
    )
```

profile of v0, /device:TPU:1, one launch (start us, length us, event | category | flops | bytes accessed | tf_op | source)
XLA Modules:
  0.0 204.2 jit_solution(13655678280055105823)
XLA Ops:
  7.2 0.0 copy-start
  7.2 0.0 reduce-scatter.2.cloned.1.call-start
  7.2 1.2 copy-done
  8.4 3.0 %convolution_convert_fusion = bf16[2048,512]{1,0:T(8,128)(2,1)} fusion(bf16[256,2048]{1,0:T(8,128)(2,1)S(1)} %copy-done, bf16[256,512]{1,0:T(8,128)(2,1)} %param.4), kind=kOutput, calls=%fused_computation | convolution fusion | flops 537919488 | bytes 3407872 | tf_op jit(solution)/shard_map/dot_general | solution.py:30
  11.4 0.0 reduce-scatter.2.cloned.1.call-update
  11.5 0.0 all-reduce.3.cloned.1.call-start
  11.5 33.2 %reduce-scatter.2.cloned.1.call-done = bf16[512,512]{1,0:T(8,128)(2,1)} async-done(((bf16[2048,512]{1,0:T(8,128)(2,1)}), bf16[512,512]{1,0:T(8,128)(2,1)}) %reduce-scatter.2.cloned.1.call-update) | async-done | bytes 524304 | tf_op jit(solution)/shard_map/reduce_scatter | solution.py:29
  44.7 2.1 %copy_bitcast_fusion = f32[512,4,128]{2,0,1:T(8,128)} fusion(bf16[512,512]{1,0:T(8,128)(2,1)} %reduce-scatter.2.cloned.1.call-done), kind=kLoop, calls=%fused_computation.13 | loop fusion | flops 262144 | bytes 1572864 | tf_op jit(solution)/shard_map/reshape | solution.py:38
  46.8 0.0 copy-start.2
  46.8 0.0 all-reduce.3.cloned.1.call-update
  46.8 0.0 all-gather.2.cloned.1.call-start
  46.8 0.7 all-gather.2.cloned.1.call-update
  47.5 0.0 all-reduce.5.cloned.1.call-start
  47.6 79.7 %all-reduce.3.cloned.1.call-done = f32[512,4,128]{2,0,1:T(8,128)} async-done(((f32[512,4,128]{2,0,1:T(8,128)}), f32[512,4,128]{2,0,1:T(8,128)}) %all-reduce.3.cloned.1.call-update) | async-done | bytes 1048592 | tf_op jit(solution)/shard_map/psum | solution.py:37
  127.3 4.1 %fusion.13 = f32[4,128,128]{2,1,0:T(8,128)} fusion(f32[512,4,128]{2,0,1:T(8,128)} %all-reduce.3.cloned.1.call-done), kind=kOutput, calls=%fused_computation.28 | convolution fusion | flops 402653184 | bytes 1310720 | tf_op jit(solution)/shard_map/rhi,rhj->hij/dot_general | solution.py:39
  131.4 0.0 all-reduce.5.cloned.1.call-update
  131.4 20.1 %all-gather.2.cloned.1.call-done = bf16[2048,512]{1,0:T(8,128)(2,1)} async-done(((bf16[512,512]{1,0:T(8,128)(2,1)}), bf16[2048,512]{1,0:T(8,128)(2,1)}) %all-gather.2.cloned.1.call-update) | async-done | bytes 2097168 | tf_op jit(solution)/shard_map/all_gather | solution.py:25
  151.5 0.0 copy-done.2
  151.5 3.3 %convolution_convert_fusion.1 = bf16[256,2048]{1,0:T(8,128)(2,1)} fusion(bf16[256,512]{1,0:T(8,128)(2,1)S(1)} %copy-done.2, bf16[2048,512]{1,0:T(8,128)(2,1)} %all-gather.2.cloned.1.call-done), kind=kOutput, calls=%fused_computation.1 | convolution fusion | flops 537395200 | bytes 3407872 | tf_op jit(solution)/shard_map/dot_general | solution.py:23
  154.8 29.8 %all-reduce.5.cloned.1.call-done = f32[4,128,128]{2,1,0:T(8,128)} async-done(((f32[4,128,128]{2,1,0:T(8,128)}), f32[4,128,128]{2,1,0:T(8,128)}) %all-reduce.5.cloned.1.call-update) | async-done | bytes 262160 | tf_op jit(solution)/shard_map/psum | solution.py:40
  184.6 0.0 copy-start.3
  184.7 1.2 select_reduce_fusion
  185.8 1.6 fusion.4
  187.4 0.4 fusion.7
  187.8 0.0 copy-done.3
  187.8 0.4 fusion.11
  188.3 0.6 fusion.14
  188.9 0.4 fusion.3
  189.2 0.4 fusion.16
  189.6 0.4 fusion.15
  190.1 0.6 fusion.17
  190.7 0.4 fusion.2
  191.0 0.4 fusion.19
  191.4 0.4 fusion.18
  191.8 0.6 fusion.20
  192.5 0.4 fusion.1
  192.8 0.0 copy-start.1
  192.8 0.4 fusion.22
  193.2 0.4 fusion.21
  193.7 0.6 fusion.23
  194.3 0.4 fusion
  194.6 0.6 fusion.24
  195.2 0.0 copy-done.1
  195.3 1.1 convolution_multiply_fusion
  196.3 1.3 copy.11
  (4 shorter events, 0.0 us)
Async XLA Ops:
  7.2 1.2 copy-start
  7.2 37.5 %reduce-scatter.2.cloned.1.call-start = ((), (), s32[]{:S(2)}) async-start(), calls=%async_computation.2 | async-start | bytes 2621440 | tf_op jit(solution)/shard_map/reduce_scatter | solution.py:29
  11.5 115.8 %all-reduce.3.cloned.1.call-start = ((), (), s32[]{:S(2)}) async-start(), calls=%async_computation.3 | async-start | bytes 2097152 | tf_op jit(solution)/shard_map/psum | solution.py:37
  46.8 104.7 %copy-start.2 = (bf16[256,512]{1,0:T(8,128)(2,1)S(1)}, bf16[256,512]{1,0:T(8,128)(2,1)}, u32[]{:S(2)}) copy-start(bf16[256,512]{1,0:T(8,128)(2,1)} %param.4) | copy-start | bytes 786436
  46.8 104.7 %all-gather.2.cloned.1.call-start = ((), (), s32[]{:S(2)}) async-start(), calls=%async_computation.1 | async-start | bytes 2621440 | tf_op jit(solution)/shard_map/all_gather | solution.py:25
  47.5 137.1 %all-reduce.5.cloned.1.call-start = ((), (), s32[]{:S(2)}) async-start(), calls=%async_computation.4 | async-start | bytes 524288 | tf_op jit(solution)/shard_map/psum | solution.py:40
  184.6 3.2 %copy-start.3 = (f32[4,128,128]{2,1,0:T(8,128)S(1)}, f32[4,128,128]{2,1,0:T(8,128)}, u32[]{:S(2)}) copy-start(f32[4,128,128]{2,1,0:T(8,128)} %all-reduce.5.cloned.1.call-done) | copy-start | bytes 786436
  192.8 2.4 %copy-start.1 = (f32[512,4,128]{2,0,1:T(8,128)S(1)}, f32[512,4,128]{2,0,1:T(8,128)}, u32[]{:S(2)}) copy-start(f32[512,4,128]{2,0,1:T(8,128)} %all-reduce.3.cloned.1.call-done) | copy-start | bytes 3145732
Sparse Core Ops, SparseCore 0:
  11.6 33.0 reduce-scatter.1
  48.8 78.4 all-reduce.2
  128.9 22.6 all-gather.1
  154.3 30.3 all-reduce.4
where the time goes:
time: 207 us; the launch traced here: 204 us
  waiting for transfers between devices  163 us (79%)
  matrix products  20.8 us (10%)
  between operations  14 us (7%)
  other arithmetic  3.28 us (2%)
  local copies, waits for them, and re-layouts  2.5 us (1%)
    psum x1, waiting for transfers between devices, per_device(): gradient = lax.psum(partial_rows, 'rep')  79.7 us
    reduce_scatter x1, waiting for transfers between devices, per_device(): lax.psum_scatter(lax.dot_general(tokens, cotangent, (((0,), (0,)), ((), (...  33.2 us
    psum x1, waiting for transfers between devices, per_device(): gram_raw = lax.psum(local_raw, 'node')  29.8 us
    all_gather x1, waiting for transfers between devices, per_device(): lax.all_gather(value_weight, 'node', axis=0, tiled=True)  20.1 us
  transfers between devices with their start and end apart: 4, of which 4 were waited for; matrix products, arithmetic and copies ran while one was open for 4% of the time, Pallas kernels for 0%

commit v1 on v0

v1 whole, which is shorter than its diff:
```python
import functools
import math

import jax
import jax.numpy as jnp
from jax import lax
from jax.experimental import pallas as pl
from jax.experimental.pallas import tpu as pltpu
from jax.sharding import PartitionSpec as P

HD = 128
NS_ITERS = 5
NSUB = 1
TILE_ROWS = 16

coef_a = 3.4445
coef_b = -4.775
coef_c = 2.0315
epsilon = 1e-07

MESH = pl.DeviceIdType.MESH
F32, BF16 = jnp.float32, jnp.bfloat16


def mm_t(a, b):
    return lax.dot_general(a, b, (((0,), (0,)), ((), ())), preferred_element_type=F32)


def parts_of(a):
    hi = a.astype(BF16)
    lo = (a - hi.astype(F32)).astype(BF16)
    return hi, lo


def left_form(a):
    return jnp.concatenate(parts_of(a), axis=1)


def right_form(b):
    row = jnp.concatenate(parts_of(b), axis=1)
    return jnp.concatenate([row, row], axis=0)


def product(left, right):
    n = right.shape[1] // 2
    wide = jnp.dot(left, right, preferred_element_type=F32)
    return wide[:, :n] + wide[:, n:]


def kernel(cfg, tok_hbm, cot_hbm, w_hbm, ig_hbm, up_hbm, tok2, cot2, wall, acc1, send1, recv1, send2, recv2,
           zsend, zrecv, grad, gram_own, gram_in, igbuf, upbuf, lsem, ssem, rsem):
    depth, width, heads, zs = cfg
    din = tok_hbm.shape[1]
    tokens = tok_hbm.shape[0]
    block = din // 4
    half, quarter = block // 2, block // 4
    piece = quarter // zs
    cw = width // NSUB

    node, rep = lax.axis_index("node"), lax.axis_index("rep")
    y, c = node // 2, node % 2
    z, x = rep // 2, rep % 2
    partner = (y * 2 + 1 - c, rep)
    y_peer = ((1 - y) * 2 + c, rep)
    x_peer = (node, z * 2 + 1 - x)
    z_of = [(z + d) % zs for d in range(zs)]
    z_peer = [(node, z_of[d] * 2 + x) for d in range(zs)]

    local_copies = {}
    counts = {"l": 0, "r": 0}

    def local(src, dst):
        cp = pltpu.make_async_copy(src, dst, lsem.at[counts["l"]])
        counts["l"] += 1
        cp.start()
        return cp

    sends = []

    def remote(src, dst, peer):
        k = counts["r"]
        counts["r"] += 1
        cp = pltpu.make_async_remote_copy(src_ref=src, dst_ref=dst, send_sem=ssem.at[k], recv_sem=rsem.at[k],
                                          device_id=peer, device_id_type=MESH)
        cp.start()
        sends.append(cp)
        return cp

    def col(p, core):
        return pl.ds(pl.multiple_of((2 * p + core) * block, block), block)

    own_rows, other_rows = pl.ds(0, tokens), pl.ds(tokens, tokens)
    loads = [local(tok_hbm.at[:, col(p, c)], tok2.at[p, own_rows]) for p in range(2)]
    loads.append(local(cot_hbm, cot2.at[own_rows]))
    own_w = pl.ds(pl.multiple_of(node * block, block), block)
    load_w = local(w_hbm, wall.at[own_w])

    barrier = pltpu.get_barrier_semaphore()
    peers = [partner, y_peer, x_peer] + z_peer[1:]
    for peer in peers:
        pl.semaphore_signal(barrier, inc=1, device_id=peer, device_id_type=MESH)
    pl.semaphore_wait(barrier, len(peers))

    first = [remote(cot_hbm, cot2.at[other_rows], partner)]
    first += [remote(tok_hbm.at[:, col(p, 1 - c)], tok2.at[p, other_rows], partner) for p in range(2)]
    w_partner = remote(w_hbm, wall.at[own_w], partner)

    def dim(p, level):
        return (y, y_peer) if (p + level) % 2 == 0 else (x, x_peer)

    chunks = [(p, s) for s in range(NSUB) for p in range(2)]

    def cs(s):
        return pl.ds(s * cw, cw)

    for cp in loads:
        cp.wait()
    for cp in first:
        cp.wait_recv()

    st1, st2, stz, sg, sg2, sg1 = {}, {}, {}, {}, {}, {}
    for p, s in chunks:
        bit, peer = dim(p, 0)
        cols = pl.ds(pl.multiple_of((1 - bit) * half, half), half)
        send1[p, :, cs(s)] = mm_t(tok2[p, :, cols], cot2[:, cs(s)]).astype(BF16)
        st1[p, s] = remote(send1.at[p, :, cs(s)], recv1.at[p, :, cs(s)], peer)
    for p, s in chunks:
        bit, peer = dim(p, 0)
        cols = pl.ds(pl.multiple_of(bit * half, half), half)
        acc1[p, :, cs(s)] = mm_t(tok2[p, :, cols], cot2[:, cs(s)])

    def input_rows(n):
        rows = pl.ds(pl.multiple_of(n * block, block), block)
        out = lax.dot_general(cot2[0:tokens], wall[rows, :], (((1,), (1,)), ((), ())), preferred_element_type=F32)
        igbuf[:, rows] = out.astype(BF16)

    load_w.wait()
    input_rows(node)
    w_partner.wait_recv()
    input_rows(y * 2 + 1 - c)

    def base(p):
        return (2 * p + c) * block

    for p, s in chunks:
        st1[p, s].wait_recv()
        bit, peer = dim(p, 1)
        away = pl.ds(pl.multiple_of((1 - bit) * quarter, quarter), quarter)
        keep = pl.ds(pl.multiple_of(bit * quarter, quarter), quarter)
        send2[p, :, cs(s)] = (acc1[p, away, cs(s)] + recv1[p, away, cs(s)].astype(F32)).astype(BF16)
        st2[p, s] = remote(send2.at[p, :, cs(s)], recv2.at[p, :, cs(s)], peer)
        acc1[p, keep, cs(s)] = acc1[p, keep, cs(s)] + recv1[p, keep, cs(s)].astype(F32)
    w_y = remote(w_hbm, wall.at[own_w], y_peer)

    for p, s in chunks:
        st2[p, s].wait_recv()
        bit, peer = dim(p, 1)
        keep = pl.ds(pl.multiple_of(bit * quarter, quarter), quarter)
        total = acc1[p, keep, cs(s)] + recv2[p, :, cs(s)].astype(F32)
        acc1[p, keep, cs(s)] = total
        zsend[p, :, cs(s)] = total.astype(BF16)
        cps = []
        for d in range(1, zs):
            rows = pl.ds(pl.multiple_of(z_of[d] * piece, piece), piece)
            cps.append(remote(zsend.at[p, rows, cs(s)], zrecv.at[p, d - 1, :, cs(s)], z_peer[d]))
        stz[p, s] = cps

    for p, s in chunks:
        b0, _ = dim(p, 0)
        b1, _ = dim(p, 1)
        mine = pl.ds(pl.multiple_of(b1 * quarter + z * piece, piece), piece)
        total = acc1[p, mine, cs(s)]
        for d in range(1, zs):
            stz[p, s][d - 1].wait_recv()
            total = total + zrecv[p, d - 1, :, cs(s)].astype(F32)
        rows = pl.ds(pl.multiple_of(b0 * half + b1 * quarter + z * piece, piece), piece)
        grad[p, rows, cs(s)] = total.astype(BF16)
        sg[p, s] = [remote(grad.at[p, rows, cs(s)], grad.at[p, rows, cs(s)], z_peer[d]) for d in range(1, zs)]

    for p, s in chunks:
        for cp in sg[p, s]:
            cp.wait_recv()
        b0, _ = dim(p, 0)
        b1, peer = dim(p, 1)
        rows = pl.ds(pl.multiple_of(b0 * half + b1 * quarter, quarter), quarter)
        sg2[p, s] = remote(grad.at[p, rows, cs(s)], grad.at[p, rows, cs(s)], peer)
    w_y.wait_recv()
    y_w = pl.ds(pl.multiple_of(((1 - y) * 2 + c) * block, block), block)
    w_fwd = remote(wall.at[y_w], wall.at[y_w], partner)
    for p, s in chunks:
        sg2[p, s].wait_recv()
        b0, peer = dim(p, 0)
        rows = pl.ds(pl.multiple_of(b0 * half, half), half)
        sg1[p, s] = remote(grad.at[p, rows, cs(s)], grad.at[p, rows, cs(s)], peer)

    input_rows((1 - y) * 2 + c)
    w_fwd.wait_recv()
    input_rows((1 - y) * 2 + 1 - c)
    store_ig = local(igbuf, ig_hbm)

    def gram_of(h, p, bit):
        rows = pl.ds(pl.multiple_of(bit * half, half), half)
        g = grad[p, rows, h * HD:(h + 1) * HD]
        return mm_t(g, g)

    for h in range(heads):
        gram_own[h] = gram_of(h, 0, y) + gram_of(h, 1, x)
    for p, s in chunks:
        sg1[p, s].wait_recv()
    for h in range(heads):
        lower = gram_of(h, 0, 0) + gram_of(h, 0, 1)
        gram_own[h] = lower + (gram_of(h, 1, 0) + gram_of(h, 1, 1))
    cp_gram = remote(gram_own, gram_in, partner)
    cp_gram.wait_recv()

    ii = lax.broadcasted_iota(jnp.int32, (HD, HD), 0)
    jj = lax.broadcasted_iota(jnp.int32, (HD, HD), 1)
    eye = (ii == jj).astype(F32)
    grams, totals, scales = [], [None] * heads, []
    for h in range(heads):
        raw = gram_own[h] + gram_in[h]
        squares = jnp.sum(jnp.sum(raw * eye, axis=1, keepdims=True), axis=0, keepdims=True)
        inverse = 1.0 / (jnp.sqrt(squares) + epsilon)
        scales.append(inverse)
        grams.append(raw * inverse * inverse)
    for step in range(NS_ITERS):
        rights = [right_form(g) for g in grams]
        squared = [product(left_form(g), r) for g, r in zip(grams, rights)]
        factors = [coef_a * eye + coef_b * g + coef_c * q for g, q in zip(grams, squared)]
        forms = [right_form(f) for f in factors]
        if step + 1 < NS_ITERS:
            halfway = [product(left_form(g), f) for g, f in zip(grams, forms)]
        if step == 0:
            totals = factors
        else:
            totals = [product(left_form(t), f) for t, f in zip(totals, forms)]
        if step + 1 < NS_ITERS:
            grams = [product(left_form(g), f) for g, f in zip(halfway, forms)]

    for h in range(heads):
        scaled = totals[h] * (scales[h] * (0.2 * math.sqrt(din)))
        form = jnp.concatenate(parts_of(scaled), axis=1)
        upbuf[:, h * HD:(h + 1) * HD] = product(grad[y, :, h * HD:(h + 1) * HD], form)
    store_up = local(upbuf, up_hbm)
    for cp in sends:
        cp.wait_send()
    store_ig.wait()
    store_up.wait()


def fused(tokens, cotangent, value_weight, zs):
    tok, din = tokens.shape
    width = cotangent.shape[1]
    heads = width // HD
    block = din // 4
    half, quarter = block // 2, block // 4
    piece = quarter // zs
    nrem = 4 + 2 * NSUB * (1 + 1 + 2 * (zs - 1) + 1 + 1) + 3
    vm = pltpu.VMEM
    return pl.pallas_call(
        functools.partial(kernel, (tok, width, heads, zs)),
        out_shape=(jax.ShapeDtypeStruct((tok, din), BF16), jax.ShapeDtypeStruct((block, width), F32)),
        in_specs=[pl.BlockSpec(memory_space=pl.ANY)] * 3,
        out_specs=(pl.BlockSpec(memory_space=pl.ANY), pl.BlockSpec(memory_space=pl.ANY)),
        scratch_shapes=[
            vm((2, 2 * tok, block), BF16),
            vm((2 * tok, width), BF16),
            vm((din, width), BF16),
            vm((2, half, width), F32),
            vm((2, half, width), BF16),
            vm((2, half, width), BF16),
            vm((2, quarter, width), BF16),
            vm((2, quarter, width), BF16),
            vm((2, quarter, width), BF16),
            vm((2, zs - 1, piece, width), BF16),
            vm((2, block, width), BF16),
            vm((heads, HD, HD), F32),
            vm((heads, HD, HD), F32),
            vm((tok, din), BF16),
            vm((block, width), F32),
            pltpu.SemaphoreType.DMA((6,)),
            pltpu.SemaphoreType.DMA((nrem,)),
            pltpu.SemaphoreType.DMA((nrem,)),
        ],
        compiler_params=pltpu.CompilerParams(collective_id=0, has_side_effects=True, vmem_limit_bytes=56 * 1024 * 1024),
    )(tokens, cotangent, value_weight)


def general(tokens, cotangent, value_weight):
    width = value_weight.shape[1]
    din = tokens.shape[1]
    local_rows = value_weight.shape[0]
    heads = width // HD
    input_grad = lax.dot_general(
        cotangent,
        lax.all_gather(value_weight, "node", axis=0, tiled=True),
        (((1,), (1,)), ((), ())),
        preferred_element_type=F32,
    ).astype(BF16)
    partial_rows = lax.psum_scatter(
        lax.dot_general(tokens, cotangent, (((0,), (0,)), ((), ())), preferred_element_type=F32).astype(BF16),
        "node",
        scatter_dimension=0,
        tiled=True,
    ).astype(F32)
    gradient = lax.psum(partial_rows, "rep")
    blocks = gradient.reshape(local_rows, heads, HD)
    exact = functools.partial(jnp.einsum, precision=lax.Precision.HIGHEST)
    gram_raw = lax.psum(exact("rhi,rhj->hij", blocks, blocks), "node")
    divisor = jnp.sqrt(jnp.einsum("hii->h", gram_raw)) + epsilon
    gram = gram_raw / (divisor * divisor)[:, None, None]
    identity = jnp.broadcast_to(jnp.eye(HD, dtype=F32), (heads, HD, HD))
    total = identity
    for step in range(NS_ITERS):
        factor = coef_a * identity + coef_b * gram + coef_c * exact("hij,hjk->hik", gram, gram)
        total = exact("hij,hjk->hik", total, factor)
        if step + 1 < NS_ITERS:
            gram = exact("hji,hjk->hik", factor, exact("hij,hjk->hik", gram, factor))
    iterate = exact("rhi,hij->rhj", blocks / divisor[None, :, None], total)
    return input_grad, 0.2 * math.sqrt(din) * iterate.reshape(local_rows, width)


def solution(mesh):
    nodes, reps = mesh.shape["node"], mesh.shape["rep"]

    def per_device(tokens, cotangent, value_weight):
        zs = reps // 2
        pieces = nodes * 4 * zs
        fits = nodes == 4 and reps % 2 == 0 and zs > 1 and tokens.shape[1] % (pieces * TILE_ROWS) == 0
        if fits:
            return fused(tokens, cotangent, value_weight, zs)
        return general(tokens, cotangent, value_weight)

    return jax.shard_map(
        per_device,
        mesh=mesh,
        in_specs=(P(("node", "rep"), None), P(("node", "rep"), None), P("node", None)),
        out_specs=(P(("node", "rep"), None), P("node", None)),
        check_vma=False,
    )
```

time: 207 us -> 53.8 us (0.26); the launches traced: 204 us -> 53.7 us
  waiting for transfers between devices: 163 us -> 0 us
  Pallas kernels: 0 us -> 49.6 us
  matrix products: 20.8 us -> 0 us
  between operations: 14 us -> 0.65 us
  other arithmetic: 3.28 us -> 0 us
    psum x2 -> x0, waiting for transfers between devices: 109 us -> none  [the longest x1 79.7 us: per_device(): gradient = lax.psum(partial_rows, 'rep')]
    pallas_call x0 -> x1, Pallas kernels: none -> 49.6 us  [fused(): pl.pallas_call(functools.partial(kernel, (tok, width, heads, zs)), out_sh...]
    reduce_scatter x1 -> x0, waiting for transfers between devices: 33.2 us -> none  [per_device(): lax.psum_scatter(lax.dot_general(tokens, cotangent, (((0,), (0,)), ((), (...]
    dot_general x22 -> x0, matrix products: 20.8 us -> none  [the longest x1 4.11 us: per_device(): jnp.einsum('rhi,rhj->hij', blocks, blocks, precision=lax.Precision.HIGHEST)]
    all_gather x1 -> x0, waiting for transfers between devices: 20.1 us -> none  [per_device(): lax.all_gather(value_weight, 'node', axis=0, tiled=True)]
    reshape x1 -> x0, other arithmetic: 2.08 us -> none  [per_device(): blocks = gradient.reshape(local_rows, heads, HD)]
  transfers between devices with their start and end apart: 4 -> 0, of which waited for: 4 -> 0; matrix products, arithmetic and copies ran while one was open for 4% -> 0% of each run, Pallas kernels for 0% -> 0%
where the time goes in v1:
time: 53.8 us; the launch traced here: 53.7 us
  Pallas kernels  49.6 us (92%)
  local copies, waits for them, and re-layouts  3.37 us (6%)
  between operations  0.65 us (1%)
    pallas_call x1, Pallas kernels, fused(): pl.pallas_call(functools.partial(kernel, (tok, width, heads, zs)), out_sh...  49.6 us
    unnamed x4, local copies, waits for them, and re-layouts  3.37 us

profile of v1, /device:TPU:1, one launch (start us, length us, event | category | flops | bytes accessed | tf_op | source)
XLA Modules:
  0.0 53.7 jit_solution(9738647816068803378)
XLA Ops:
  0.6 49.6 %shard_map.50 = (bf16[256,2048]{1,0:T(8,128)(2,1)}, f32[512,512]{1,0:T(8,128)}) custom-call(bf16[256,2048]{1,0:T(8,128)(2,1)} %tok_hbm.1, bf16[256,512]{1,0:T(8,128)(2,1)} %cot_hbm.1, bf16[512,512]{1,0:T(8,128)(2,1)} %w_hbm.1), custom_call_target="tpu_custom_call" | custom-call | tf_op jit(solution)/shard_map/pallas_call | solution.py:260
  50.3 0.0 copy-start
  50.3 2.4 %copy.7 = bf16[256,2048]{1,0:T(8,128)(2,1)} copy(bf16[256,2048]{1,0:T(8,128)(2,1)} %get-tuple-element.4) | data formatting | bytes 2097152
  52.7 0.0 copy-done
  52.7 1.0 %copy.8 = f32[512,512]{1,0:T(8,128)} copy(f32[512,512]{1,0:T(8,128)S(1)} %copy-done) | data formatting | bytes 2097152
Async XLA Ops:
  50.3 2.4 %copy-start = (f32[512,512]{1,0:T(8,128)S(1)}, f32[512,512]{1,0:T(8,128)}, u32[]{:S(2)}) copy-start(f32[512,512]{1,0:T(8,128)} %get-tuple-element.5) | copy-start | bytes 3145732

commit v2 on v1

--- a/solution.py
+++ b/solution.py
@@ -10,7 +10,7 @@
 
 HD = 128
 NS_ITERS = 5
-NSUB = 1
+NSUB = 2
 TILE_ROWS = 16
 
 coef_a = 3.4445
@@ -47,11 +47,11 @@
     return wide[:, :n] + wide[:, n:]
 
 
-def kernel(cfg, tok_hbm, cot_hbm, w_hbm, ig_hbm, up_hbm, tok2, cot2, wall, acc1, send1, recv1, send2, recv2,
-           zsend, zrecv, grad, gram_own, gram_in, igbuf, upbuf, lsem, ssem, rsem):
+def kernel(cfg, tok_hbm, cot_hbm, w_hbm, igbuf, rows_ref, form_ref, tok_ref, cot_ref, w_ref, tokx, cotx, wall, acc1, away1, send1, recv1, send2,
+           recv2, zsend, zrecv, grad, early, gram_own, gram_in, lsem, ssem, rsem):
     depth, width, heads, zs = cfg
-    din = tok_hbm.shape[1]
-    tokens = tok_hbm.shape[0]
+    din = tok_ref.shape[1]
+    tokens = tok_ref.shape[0]
     block = din // 4
     half, quarter = block // 2, block // 4
     piece = quarter // zs
@@ -66,34 +66,27 @@
     z_of = [(z + d) % zs for d in range(zs)]
     z_peer = [(node, z_of[d] * 2 + x) for d in range(zs)]
 
-    local_copies = {}
-    counts = {"l": 0, "r": 0}
-
-    def local(src, dst):
-        cp = pltpu.make_async_copy(src, dst, lsem.at[counts["l"]])
-        counts["l"] += 1
-        cp.start()
-        return cp
-
+    counts = [0]
     sends = []
 
     def remote(src, dst, peer):
-        k = counts["r"]
-        counts["r"] += 1
+        k = counts[0]
+        counts[0] += 1
         cp = pltpu.make_async_remote_copy(src_ref=src, dst_ref=dst, send_sem=ssem.at[k], recv_sem=rsem.at[k],
                                           device_id=peer, device_id_type=MESH)
         cp.start()
         sends.append(cp)
         return cp
 
-    def col(p, core):
-        return pl.ds(pl.multiple_of((2 * p + core) * block, block), block)
-
-    own_rows, other_rows = pl.ds(0, tokens), pl.ds(tokens, tokens)
-    loads = [local(tok_hbm.at[:, col(p, c)], tok2.at[p, own_rows]) for p in range(2)]
-    loads.append(local(cot_hbm, cot2.at[own_rows]))
+    def col(p, core, start=0, size=block):
+        return pl.ds(pl.multiple_of((2 * p + core) * block + start, size), size)
+
     own_w = pl.ds(pl.multiple_of(node * block, block), block)
-    load_w = local(w_hbm, wall.at[own_w])
+
+    pairs = ((cot_hbm, cot_ref), (tok_hbm, tok_ref), (w_hbm, w_ref))
+    loads = [pltpu.make_async_copy(src, dst, lsem.at[i]) for i, (src, dst) in enumerate(pairs)]
+    for cp in loads:
+        cp.start()
 
     barrier = pltpu.get_barrier_semaphore()
     peers = [partner, y_peer, x_peer] + z_peer[1:]
@@ -101,9 +94,23 @@
         pl.semaphore_signal(barrier, inc=1, device_id=peer, device_id_type=MESH)
     pl.semaphore_wait(barrier, len(peers))
 
-    first = [remote(cot_hbm, cot2.at[other_rows], partner)]
-    first += [remote(tok_hbm.at[:, col(p, 1 - c)], tok2.at[p, other_rows], partner) for p in range(2)]
-    w_partner = remote(w_hbm, wall.at[own_w], partner)
+    for cp in loads:
+        cp.wait()
+    first = [remote(cot_ref, cotx, partner)]
+    first += [remote(tok_ref.at[:, col(p, 1 - c)], tokx.at[p], partner) for p in range(2)]
+
+    def w_part(n, side, i):
+        return pl.ds(pl.multiple_of(n * block + side * half + i * quarter, quarter), quarter)
+
+    def send_w(i):
+        rows = pl.ds(pl.multiple_of(x * half + i * quarter, quarter), quarter)
+        return remote(w_ref.at[rows], wall.at[w_part(node, x, i)], y_peer)
+
+    def relay_w(i):
+        rows = w_part((1 - y) * 2 + c, x, i)
+        return remote(wall.at[rows], wall.at[rows], x_peer)
+
+    w_y = [send_w(0)]
 
     def dim(p, level):
         return (y, y_peer) if (p + level) % 2 == 0 else (x, x_peer)
@@ -113,34 +120,37 @@
     def cs(s):
         return pl.ds(s * cw, cw)
 
-    for cp in loads:
-        cp.wait()
-    for cp in first:
-        cp.wait_recv()
-
+    def chip_sum(p, start):
+        mine = mm_t(tok_ref[:, col(p, c, start, half)], cot_ref[...])
+        return mine, pl.ds(pl.multiple_of(start, half), half)
+
+    mine = {}
+    for p in range(2):
+        start = (1 - dim(p, 0)[0]) * half
+        away1[p], mine[p] = chip_sum(p, start)
     st1, st2, stz, sg, sg2, sg1 = {}, {}, {}, {}, {}, {}
-    for p, s in chunks:
-        bit, peer = dim(p, 0)
-        cols = pl.ds(pl.multiple_of((1 - bit) * half, half), half)
-        send1[p, :, cs(s)] = mm_t(tok2[p, :, cols], cot2[:, cs(s)]).astype(BF16)
-        st1[p, s] = remote(send1.at[p, :, cs(s)], recv1.at[p, :, cs(s)], peer)
-    for p, s in chunks:
-        bit, peer = dim(p, 0)
-        cols = pl.ds(pl.multiple_of(bit * half, half), half)
-        acc1[p, :, cs(s)] = mm_t(tok2[p, :, cols], cot2[:, cs(s)])
-
-    def input_rows(n):
+    first[0].wait_recv()
+    for p in range(2):
+        first[1 + p].wait_recv()
+        send1[p] = (away1[p] + mm_t(tokx[p, :, mine[p]], cotx[...])).astype(BF16)
+        for s in range(NSUB):
+            st1[p, s] = remote(send1.at[p, :, cs(s)], recv1.at[p, :, cs(s)], dim(p, 0)[1])
+    w_partner = remote(w_ref, wall.at[own_w], partner)
+    for p in range(2):
+        value, here = chip_sum(p, dim(p, 0)[0] * half)
+        acc1[p] = value + mm_t(tokx[p, :, here], cotx[...])
+
+    def input_rows(n, rows_of_w):
         rows = pl.ds(pl.multiple_of(n * block, block), block)
-        out = lax.dot_general(cot2[0:tokens], wall[rows, :], (((1,), (1,)), ((), ())), preferred_element_type=F32)
+        out = lax.dot_general(cot_ref[...], rows_of_w, (((1,), (1,)), ((), ())), preferred_element_type=F32)
         igbuf[:, rows] = out.astype(BF16)
 
-    load_w.wait()
-    input_rows(node)
+    def gathered(n):
+        return wall[pl.ds(pl.multiple_of(n * block, block), block), :]
+
+    input_rows(node, w_ref[...])
     w_partner.wait_recv()
-    input_rows(y * 2 + 1 - c)
-
-    def base(p):
-        return (2 * p + c) * block
+    input_rows(y * 2 + 1 - c, gathered(y * 2 + 1 - c))
 
     for p, s in chunks:
         st1[p, s].wait_recv()
@@ -150,7 +160,9 @@
         send2[p, :, cs(s)] = (acc1[p, away, cs(s)] + recv1[p, away, cs(s)].astype(F32)).astype(BF16)
         st2[p, s] = remote(send2.at[p, :, cs(s)], recv2.at[p, :, cs(s)], peer)
         acc1[p, keep, cs(s)] = acc1[p, keep, cs(s)] + recv1[p, keep, cs(s)].astype(F32)
-    w_y = remote(w_hbm, wall.at[own_w], y_peer)
+    w_y.append(send_w(1))
+    w_y[0].wait_recv()
+    w_x = [relay_w(0)]
 
     for p, s in chunks:
         st2[p, s].wait_recv()
@@ -177,6 +189,8 @@
         grad[p, rows, cs(s)] = total.astype(BF16)
         sg[p, s] = [remote(grad.at[p, rows, cs(s)], grad.at[p, rows, cs(s)], z_peer[d]) for d in range(1, zs)]
 
+    w_y[1].wait_recv()
+    w_x.append(relay_w(1))
     for p, s in chunks:
         for cp in sg[p, s]:
             cp.wait_recv()
@@ -184,7 +198,8 @@
         b1, peer = dim(p, 1)
         rows = pl.ds(pl.multiple_of(b0 * half + b1 * quarter, quarter), quarter)
         sg2[p, s] = remote(grad.at[p, rows, cs(s)], grad.at[p, rows, cs(s)], peer)
-    w_y.wait_recv()
+    for cp in w_x:
+        cp.wait_recv()
     y_w = pl.ds(pl.multiple_of(((1 - y) * 2 + c) * block, block), block)
     w_fwd = remote(wall.at[y_w], wall.at[y_w], partner)
     for p, s in chunks:
@@ -193,10 +208,9 @@
         rows = pl.ds(pl.multiple_of(b0 * half, half), half)
         sg1[p, s] = remote(grad.at[p, rows, cs(s)], grad.at[p, rows, cs(s)], peer)
 
-    input_rows((1 - y) * 2 + c)
+    input_rows((1 - y) * 2 + c, gathered((1 - y) * 2 + c))
     w_fwd.wait_recv()
-    input_rows((1 - y) * 2 + 1 - c)
-    store_ig = local(igbuf, ig_hbm)
+    input_rows((1 - y) * 2 + 1 - c, gathered((1 - y) * 2 + 1 - c))
 
     def gram_of(h, p, bit):
         rows = pl.ds(pl.multiple_of(bit * half, half), half)
@@ -204,13 +218,14 @@
         return mm_t(g, g)
 
     for h in range(heads):
-        gram_own[h] = gram_of(h, 0, y) + gram_of(h, 1, x)
+        early[0, h] = gram_of(h, 0, y)
+        early[1, h] = gram_of(h, 1, x)
     for p, s in chunks:
         sg1[p, s].wait_recv()
     for h in range(heads):
-        lower = gram_of(h, 0, 0) + gram_of(h, 0, 1)
-        gram_own[h] = lower + (gram_of(h, 1, 0) + gram_of(h, 1, 1))
+        gram_own[h] = (early[0, h] + gram_of(h, 0, 1 - y)) + (early[1, h] + gram_of(h, 1, 1 - x))
     cp_gram = remote(gram_own, gram_in, partner)
+    rows_ref[...] = grad[y]
     cp_gram.wait_recv()
 
     ii = lax.broadcasted_iota(jnp.int32, (HD, HD), 0)
@@ -239,13 +254,25 @@
 
     for h in range(heads):
         scaled = totals[h] * (scales[h] * (0.2 * math.sqrt(din)))
-        form = jnp.concatenate(parts_of(scaled), axis=1)
-        upbuf[:, h * HD:(h + 1) * HD] = product(grad[y, :, h * HD:(h + 1) * HD], form)
-    store_up = local(upbuf, up_hbm)
+        form_ref[h] = jnp.concatenate(parts_of(scaled), axis=1)
     for cp in sends:
         cp.wait_send()
-    store_ig.wait()
-    store_up.wait()
+
+
+def finish(ig_ref, rows_ref, form_ref, ig_out, up_out, upbuf, sems):
+    heads = form_ref.shape[0]
+    step = upbuf.shape[0] // 4
+    copies = [pltpu.make_async_copy(ig_ref, ig_out, sems.at[0])]
+    copies[0].start()
+    for i in range(4):
+        part = pl.ds(i * step, step)
+        for h in range(heads):
+            cols = pl.ds(h * HD, HD)
+            upbuf[part, cols] = product(rows_ref[part, cols], form_ref[h])
+        copies.append(pltpu.make_async_copy(upbuf.at[part], up_out.at[part], sems.at[i + 1]))
+        copies[-1].start()
+    for cp in copies:
+        cp.wait()
 
 
 def fused(tokens, cotangent, value_weight, zs):
@@ -255,17 +282,25 @@
     block = din // 4
     half, quarter = block // 2, block // 4
     piece = quarter // zs
-    nrem = 4 + 2 * NSUB * (1 + 1 + 2 * (zs - 1) + 1 + 1) + 3
+    nrem = 4 + 2 * NSUB * (1 + 1 + 2 * (zs - 1) + 1 + 1) + 7
     vm = pltpu.VMEM
-    return pl.pallas_call(
+    held = pl.pallas_call(
         functools.partial(kernel, (tok, width, heads, zs)),
-        out_shape=(jax.ShapeDtypeStruct((tok, din), BF16), jax.ShapeDtypeStruct((block, width), F32)),
+        out_shape=(
+            jax.ShapeDtypeStruct((tok, din), BF16),
+            jax.ShapeDtypeStruct((block, width), BF16),
+            jax.ShapeDtypeStruct((heads, HD, 2 * HD), BF16),
+        ),
         in_specs=[pl.BlockSpec(memory_space=pl.ANY)] * 3,
-        out_specs=(pl.BlockSpec(memory_space=pl.ANY), pl.BlockSpec(memory_space=pl.ANY)),
+        out_specs=(pl.BlockSpec(memory_space=pltpu.VMEM),) * 3,
         scratch_shapes=[
-            vm((2, 2 * tok, block), BF16),
-            vm((2 * tok, width), BF16),
+            vm((tok, din), BF16),
+            vm((tok, width), BF16),
+            vm((block, width), BF16),
+            vm((2, tok, block), BF16),
+            vm((tok, width), BF16),
             vm((din, width), BF16),
+            vm((2, half, width), F32),
             vm((2, half, width), F32),
             vm((2, half, width), BF16),
             vm((2, half, width), BF16),
@@ -274,16 +309,23 @@
             vm((2, quarter, width), BF16),
             vm((2, zs - 1, piece, width), BF16),
             vm((2, block, width), BF16),
+            vm((2, heads, HD, HD), F32),
             vm((heads, HD, HD), F32),
             vm((heads, HD, HD), F32),
-            vm((tok, din), BF16),
-            vm((block, width), F32),
-            pltpu.SemaphoreType.DMA((6,)),
+            pltpu.SemaphoreType.DMA((3,)),
             pltpu.SemaphoreType.DMA((nrem,)),
             pltpu.SemaphoreType.DMA((nrem,)),
         ],
-        compiler_params=pltpu.CompilerParams(collective_id=0, has_side_effects=True, vmem_limit_bytes=56 * 1024 * 1024),
-    )(tokens, cotangent, value_weight)
+        compiler_params=pltpu.CompilerParams(collective_id=0, has_side_effects=True, vmem_limit_bytes=24 * 1024 * 1024),
+    )(*(pltpu.with_memory_space_constraint(a, pltpu.HBM) for a in (tokens, cotangent, value_weight)))
+    return pl.pallas_call(
+        finish,
+        out_shape=(jax.ShapeDtypeStruct((tok, din), BF16), jax.ShapeDtypeStruct((block, width), F32)),
+        in_specs=[pl.BlockSpec(memory_space=pltpu.VMEM)] * 3,
+        out_specs=(pl.BlockSpec(memory_space=pltpu.HBM),) * 2,
+        scratch_shapes=[vm((block, width), F32), pltpu.SemaphoreType.DMA((5,))],
+        compiler_params=pltpu.CompilerParams(vmem_limit_bytes=8 * 1024 * 1024),
+    )(*held)
 
 
 def general(tokens, cotangent, value_weight):

time: 53.8 us -> 45.1 us (0.84)
  Pallas kernels: 49.6 us -> 44.3 us
  local copies, waits for them, and re-layouts: 3.37 us -> 0 us
    pallas_call x1, Pallas kernels: 49.6 us -> 42.9 us  [fused(): pl.pallas_call(functools.partial(kernel, (tok, width, heads, zs)), out_sh...]
    unnamed x4 -> x0, local copies, waits for them, and re-layouts: 3.37 us -> none
    pallas_call x0 -> x1, Pallas kernels: none -> 1.36 us  [fused(): pl.pallas_call(finish, out_shape=(jax.ShapeDtypeStruct((tok, din), BF16),...]
where the time goes in v2:
time: 45.1 us; the launch traced here: 44.9 us
  Pallas kernels  44.3 us (98%)
  between operations  0.64 us (1%)
    pallas_call x1, Pallas kernels, fused(): pl.pallas_call(functools.partial(kernel, (tok, width, heads, zs)), out_sh...  42.9 us
    pallas_call x1, Pallas kernels, fused(): pl.pallas_call(finish, out_shape=(jax.ShapeDtypeStruct((tok, din), BF16),...  1.36 us

profile of v2, /device:TPU:1, one launch (start us, length us, event | category | flops | bytes accessed | tf_op | source)
XLA Modules:
  0.0 44.9 jit_solution(11494161731837456555)
XLA Ops:
  0.6 42.9 %shard_map.50 = (bf16[256,2048]{1,0:T(8,128)(2,1)S(1)}, bf16[512,512]{1,0:T(8,128)(2,1)S(1)}, bf16[4,128,256]{2,1,0:T(8,128)(2,1)S(1)}) custom-call(bf16[256,2048]{1,0:T(8,128)(2,1)} %tok_hbm.1, bf16[256,512]{1,0:T(8,128)(2,1)} %cot_hbm.1, bf16[512,512]{1,0:T(8,128)(2,1)} %w_hbm.1), custom_call_target="tpu_custom_call" | custom-call | tf_op jit(solution)/shard_map/pallas_call | solution.py:287
  43.6 1.4 %shard_map.51 = (bf16[256,2048]{1,0:T(8,128)(2,1)}, f32[512,512]{1,0:T(8,128)}) custom-call(bf16[256,2048]{1,0:T(8,128)(2,1)S(1)} %get-tuple-element.5.ig_ref, bf16[512,512]{1,0:T(8,128)(2,1)S(1)} %get-tuple-element.6.rows_ref, bf16[4,128,256]{2,1,0:T(8,128)(2,1)S(1)} %get-tuple-element.7.form_ref), custom_call_target="tpu_custom_call" | custom-call | tf_op jit(solution)/shard_map/pallas_call | solution.py:321

commit v3 on v2

--- a/solution.py
+++ b/solution.py
@@ -94,7 +94,7 @@
         pl.semaphore_signal(barrier, inc=1, device_id=peer, device_id_type=MESH)
     pl.semaphore_wait(barrier, len(peers))
 
-    for cp in loads:
+    for cp in loads[:2]:
         cp.wait()
     first = [remote(cot_ref, cotx, partner)]
     first += [remote(tok_ref.at[:, col(p, 1 - c)], tokx.at[p], partner) for p in range(2)]
@@ -110,6 +110,7 @@
         rows = w_part((1 - y) * 2 + c, x, i)
         return remote(wall.at[rows], wall.at[rows], x_peer)
 
+    loads[2].wait()
     w_y = [send_w(0)]
 
     def dim(p, level):
@@ -220,13 +221,18 @@
     for h in range(heads):
         early[0, h] = gram_of(h, 0, y)
         early[1, h] = gram_of(h, 1, x)
-    for p, s in chunks:
-        sg1[p, s].wait_recv()
-    for h in range(heads):
-        gram_own[h] = (early[0, h] + gram_of(h, 0, 1 - y)) + (early[1, h] + gram_of(h, 1, 1 - x))
-    cp_gram = remote(gram_own, gram_in, partner)
+    per_sub = heads // NSUB
+    cp_gram = []
+    for s in range(NSUB):
+        for p in range(2):
+            sg1[p, s].wait_recv()
+        for h in range(s * per_sub, (s + 1) * per_sub):
+            gram_own[h] = (early[0, h] + gram_of(h, 0, 1 - y)) + (early[1, h] + gram_of(h, 1, 1 - x))
+        these = pl.ds(s * per_sub, per_sub)
+        cp_gram.append(remote(gram_own.at[these], gram_in.at[these], partner))
     rows_ref[...] = grad[y]
-    cp_gram.wait_recv()
+    for cp in cp_gram:
+        cp.wait_recv()
 
     ii = lax.broadcasted_iota(jnp.int32, (HD, HD), 0)
     jj = lax.broadcasted_iota(jnp.int32, (HD, HD), 1)
@@ -282,7 +288,7 @@
     block = din // 4
     half, quarter = block // 2, block // 4
     piece = quarter // zs
-    nrem = 4 + 2 * NSUB * (1 + 1 + 2 * (zs - 1) + 1 + 1) + 7
+    nrem = 4 + 2 * NSUB * (1 + 1 + 2 * (zs - 1) + 1 + 1) + 6 + NSUB
     vm = pltpu.VMEM
     held = pl.pallas_call(
         functools.partial(kernel, (tok, width, heads, zs)),

time: 45.1 us -> 44.7 us (level)
  no operation moved by 1% of the time
where the time goes in v3:
time: 44.7 us; the launch traced here: 44.5 us
  Pallas kernels  43.9 us (98%)
  between operations  0.64 us (1%)
    pallas_call x1, Pallas kernels, fused(): pl.pallas_call(functools.partial(kernel, (tok, width, heads, zs)), out_sh...  42.5 us
    pallas_call x1, Pallas kernels, fused(): pl.pallas_call(finish, out_shape=(jax.ShapeDtypeStruct((tok, din), BF16),...  1.36 us

profile of v3, /device:TPU:1, one launch (start us, length us, event | category | flops | bytes accessed | tf_op | source)
XLA Modules:
  0.0 44.5 jit_solution(10596087759508469810)
XLA Ops:
  0.6 42.5 %shard_map.50 = (bf16[256,2048]{1,0:T(8,128)(2,1)S(1)}, bf16[512,512]{1,0:T(8,128)(2,1)S(1)}, bf16[4,128,256]{2,1,0:T(8,128)(2,1)S(1)}) custom-call(bf16[256,2048]{1,0:T(8,128)(2,1)} %tok_hbm.1, bf16[256,512]{1,0:T(8,128)(2,1)} %cot_hbm.1, bf16[512,512]{1,0:T(8,128)(2,1)} %w_hbm.1), custom_call_target="tpu_custom_call" | custom-call | tf_op jit(solution)/shard_map/pallas_call | solution.py:293
  43.2 1.4 %shard_map.51 = (bf16[256,2048]{1,0:T(8,128)(2,1)}, f32[512,512]{1,0:T(8,128)}) custom-call(bf16[256,2048]{1,0:T(8,128)(2,1)S(1)} %get-tuple-element.5.ig_ref, bf16[512,512]{1,0:T(8,128)(2,1)S(1)} %get-tuple-element.6.rows_ref, bf16[4,128,256]{2,1,0:T(8,128)(2,1)S(1)} %get-tuple-element.7.form_ref), custom_call_target="tpu_custom_call" | custom-call | tf_op jit(solution)/shard_map/pallas_call | solution.py:327
